TPU v7x, 32 devices: a whole 2x2x4 slice. The times are simulated.
32 devices in a mesh: dp: 4 (over z), head: 8 (over y, x, core).
Axes of the slice: x: 2, y: 2, z: 4, core: 2. Of those that a mesh axis runs over, the one named last changes fastest.
Arguments:
- projected: bfloat16 [12288, 24576], P(('dp', 'head')), may hold values from -64 to 64, as said below
- weight_exp: int32 [12288], P(('dp', 'head')), may hold values from 0 to 3
- damp_exp: int32 [128], replicated, may hold values from 0 to 2
Outputs:
- whitening: float32 [128, 192, 192], P('head')
Inputs may be any that keep to these rules, and one draw needn't show every extreme that they name: `projected`: real values.
All inputs are finite; a program needn't handle non-finite values.
Results may differ from a plain program's by a relative error of at most 0.0003.
Values may be sent and summed in bfloat16 or wider, within the bound.
A program may use at most 192 MiB of HBM per device.

v0:
```python
import functools

import jax
import jax.numpy as jnp
from jax import lax
from jax.experimental import pallas as pl
from jax.experimental.pallas import tpu as pltpu
from jax.sharding import PartitionSpec as P

HD = 192
BLK = HD // 3
HIGH = lax.Precision.HIGHEST


def store_pair(rows, wide, out, at):
    weighted = rows * wide
    contract = (((0,), (0,)), ((), ()))
    width = 4 * BLK
    first = lax.dot_general(rows[:, :width], weighted[:, :width], contract, preferred_element_type=jnp.float32)
    second = lax.dot_general(rows[:, -width:], weighted[:, -width:], contract, preferred_element_type=jnp.float32)
    two = 2 * BLK
    lanes = lax.broadcasted_iota(jnp.int32, (BLK, two), 1)
    corner = pltpu.roll(first[two : two + BLK, two:], BLK, 1)
    out[at, :BLK, :] = jnp.where(lanes < BLK, first[:BLK, :two], corner)
    out[at, BLK:, :] = first[BLK:HD, :two]
    out[at + 1, :two, :] = second[BLK : BLK + two, two:]
    corner = pltpu.roll(second[BLK:two, :two], BLK, 1)
    out[at + 1, two:, :] = jnp.where(lanes < BLK, corner, second[HD:, two:])


def dot(a, b):
    return lax.dot_general(a, b, (((1,), (0,)), ((), ())), precision=HIGH, preferred_element_type=jnp.float32)


def dot_t(a, b):
    return lax.dot_general(a, b, (((1,), (1,)), ((), ())), precision=HIGH, preferred_element_type=jnp.float32)


def inverse_factors(blocks):
    lane = lax.broadcasted_iota(jnp.int32, (8, BLK), 1)
    sub = lax.broadcasted_iota(jnp.int32, (8, BLK), 0)
    sub1 = lax.broadcasted_iota(jnp.int32, (8, 1), 0)
    groups = BLK // 8
    held = [[block[8 * g : 8 * g + 8] for g in range(groups)] for block in blocks]
    for k in range(BLK):
        own, spot = divmod(k, 8)
        is_k = lane == k
        for parts in held:
            row = parts[own][spot : spot + 1, :]
            scale = 1.0 / row[:, k : k + 1]
            row = jnp.where(is_k[:1], 1.0, row) * scale
            for g in range(own, groups):
                part = parts[g]
                column = part[:, k : k + 1]
                if g == own:
                    if spot == 7:
                        continue
                    column = jnp.where(sub1 > spot, column, 0.0)
                    kept = jnp.where(is_k & (sub > spot), 0.0, part)
                else:
                    kept = jnp.where(is_k, 0.0, part)
                parts[g] = kept - column * row
    out = []
    for parts in held:
        rows = []
        for g in range(groups):
            ids = sub + 8 * g
            pivot = jnp.sum(jnp.where(lane == ids, parts[g], 0.0), axis=1, keepdims=True)
            unit = jnp.where(lane < ids, parts[g], jnp.where(lane == ids, 1.0, 0.0))
            rows.append(unit * (1.0 / jnp.sqrt(pivot)))
        out.append(jnp.concatenate(rows, axis=0))
    return out


def unpack_even(got):
    two = 2 * BLK
    return got[:BLK, :BLK], got[BLK:two, BLK:], got[:BLK, BLK:], got[BLK:, :BLK], got[two:, BLK:]


def unpack_odd(got):
    two = 2 * BLK
    return got[two:, :BLK], got[BLK:two, :BLK], got[two:, BLK:], got[:BLK, :].T, got[BLK:two, BLK:].T


def whiten_kernel(total, count, damp_ref, packed_ref, out_ref):
    two = 2 * BLK
    diag = lax.broadcasted_iota(jnp.int32, (BLK, BLK), 0) == lax.broadcasted_iota(jnp.int32, (BLK, BLK), 1)
    a11, a22, a33, low, a32 = [], [], [], [], []
    for m in range(count):
        got = packed_ref[m] / total
        even = unpack_even(got)
        odd = unpack_odd(got)
        if count % 2 == 0:
            d1, d2, d3, left, corner = odd if m % 2 else even
        else:
            turn = (lax.axis_index("head") * lax.axis_size("dp") + lax.axis_index("dp")) * count + m
            d1, d2, d3, left, corner = (jnp.where(turn % 2 == 0, a, b) for a, b in zip(even, odd))
        trace = jnp.sum(jnp.where(diag, d1 + d2 + d3, 0.0), axis=(0, 1), keepdims=True)
        level = trace / HD + 1e-06
        shift = jnp.where(diag, damp_ref[m] * level, 0.0)
        a11.append(d1 + shift)
        a22.append(d2 + shift)
        a33.append(d3 + shift)
        low.append(left)
        a32.append(corner)
    each = range(count)
    w11 = inverse_factors(a11)
    l1 = [dot_t(low[m], w11[m]) for m in each]
    square = [dot_t(l1[m], l1[m]) for m in each]
    w22 = inverse_factors([a22[m] - square[m][:BLK, :BLK] for m in each])
    l32 = [dot_t(a32[m] - square[m][BLK:, :BLK], w22[m]) for m in each]
    w33 = inverse_factors([a33[m] - square[m][BLK:, BLK:] - dot_t(l32[m], l32[m]) for m in each])
    for m in each:
        below = dot(l1[m], w11[m])
        w21 = -dot(w22[m], below[:BLK])
        w32 = -dot(w33[m], dot(l32[m], w22[m]))
        w31 = -dot(w33[m], below[BLK:] + dot(l32[m], w21))
        out_ref[m, :BLK] = jnp.concatenate((w11[m], w33[m]), axis=1)
        out_ref[m, BLK:two] = jnp.concatenate((w21, w22[m]), axis=1)
        out_ref[m, two:] = jnp.concatenate((w31, w32), axis=1)


def whiten(packed, damp, total):
    count = packed.shape[0]
    return pl.pallas_call(
        functools.partial(whiten_kernel, total, count),
        in_specs=[pl.BlockSpec(memory_space=pltpu.SMEM), pl.BlockSpec(memory_space=pltpu.VMEM)],
        out_specs=pl.BlockSpec(memory_space=pltpu.VMEM),
        out_shape=jax.ShapeDtypeStruct(packed.shape, jnp.float32),
    )(damp, packed)


def flip(index, step):
    return index + step * (1 - 2 * ((index // step) % 2))


def remote(src, dst, sems, slot, device):
    return pltpu.make_async_remote_copy(
        src_ref=src,
        dst_ref=dst,
        send_sem=sems.at[0, slot],
        recv_sem=sems.at[1, slot],
        device_id=device,
        device_id_type=pl.DeviceIdType.MESH,
    )


def greet(heads, dps):
    barrier = pltpu.get_barrier_semaphore()
    for peer in heads:
        pl.semaphore_signal(barrier, inc=1, device_id={"head": peer}, device_id_type=pl.DeviceIdType.MESH)
    for peer in dps:
        pl.semaphore_signal(barrier, inc=1, device_id={"dp": peer}, device_id_type=pl.DeviceIdType.MESH)
    pl.semaphore_wait(barrier, len(heads) + len(dps))


def part_rows():
    last = HD // 4
    first = (HD - last) // 2
    return (0, first), (first, first), (2 * first, last)


def scatter_kernel(n_head, n_dp, share, rows_ref, weights_ref, out_ref, acc, sent, own_grams, wide, columns, got_a, got_b, got_c, got_z, got_y, sem_in, sem_0, sem_a, sem_b, sem_c, sem_z, sem_y):
    head = lax.axis_index("head")
    dp = lax.axis_index("dp")
    chunks = n_head // 2
    bits = chunks.bit_length() - 1
    mine = head // 2
    core = head % 2
    per_head = share * n_dp
    span = per_head * HD
    peers = [lax.rem(dp + o, n_dp) for o in range(1, n_dp)]
    part_a, part_b, part_c = part_rows()
    up = list(range(bits))
    down = up[::-1]
    rows_c = pl.ds(part_c[0], part_c[1])

    def chunk_of(e):
        chunk = mine
        for j in range(bits):
            if (e >> j) & 1:
                chunk = chunk + (1 - 2 * ((mine // (1 << j)) % 2)) * (1 << j)
        return chunk

    order = list(range(chunks))[::-1]
    visits = []
    for e in order:
        visits += [2 * chunk_of(e) + 1 - core, 2 * chunk_of(e) + core]

    def fetch(v):
        start = pl.multiple_of(visits[v] * span, 2 * BLK)
        return pltpu.make_async_copy(rows_ref.at[:, pl.ds(start, span)], columns.at[v % 2], sem_in.at[v % 2])

    fetch(0).start()
    wide[...] = jnp.broadcast_to(weights_ref[...], wide.shape)
    greet([flip(head, 1 << j) for j in range(bits + 1)], peers)

    def multiply(v, out):
        if v + 1 < len(visits):
            fetch(v + 1).start()
        fetch(v).wait()

        def pair(i, carry):
            start = pl.multiple_of(i * 2 * HD, 2 * BLK)
            store_pair(columns[v % 2, :, pl.ds(start, 2 * HD)], wide[...], out, 2 * i)
            return carry

        lax.fori_loop(0, per_head // 2, pair, 0, unroll=2)

    def squeeze(e, j):
        return (e >> (j + 1) << j) | (e & ((1 << j) - 1))

    early = {"a": [], "b": []}
    flight_z = []
    for n, e in enumerate(order):
        c = chunk_of(e)
        multiply(2 * n, sent.at[n])
        copy = remote(sent.at[n], acc.at[c], sem_0, n, {"head": flip(head, 1)})
        copy.start()
        multiply(2 * n + 1, own_grams)
        copy.wait()

        def add(m, carry, c=c):
            acc[c, m] += own_grams[m]
            return carry

        lax.fori_loop(0, per_head, add, 0)
        for name, (start, size), got, sems, j in (("a", part_a, got_a, sem_a, up[0]), ("b", part_b, got_b, sem_b, down[0])):
            if (e >> j) & 1:
                slot = squeeze(e, j)
                out = remote(
                    acc.at[c, pl.ds(0, per_head), pl.ds(start, size)], got.at[slot], sems, slot, {"head": flip(head, 2 << j)}
                )
                out.start()
                early[name].append((out, chunk_of(e ^ (1 << j)), slot))
        for o, peer in enumerate(peers):
            out = remote(
                acc.at[c, pl.ds(peer * share, share), rows_c], got_z.at[o, e], sem_z, o * chunks + e, {"dp": peer}
            )
            out.start()
            flight_z.append(out)

    def begin(part, got, sems, order, step, first, count):
        j = order[step]
        bit = (mine // (1 << j)) % 2
        fixed = 0
        for done in order[:step]:
            fixed = fixed + (mine // (1 << done)) % 2 * (1 << done)
        free = [b for b in range(bits) if b not in order[: step + 1]]
        flight = []
        start, size = part
        offset = sum(chunks >> (s + 1) for s in range(step))
        for e in range(1 << len(free)):
            base = fixed + sum(((e >> i) & 1) << b for i, b in enumerate(free))
            slot = offset + e
            copy = remote(
                acc.at[base + (1 - bit) * (1 << j), pl.ds(first, count), pl.ds(start, size)],
                got.at[slot],
                sems,
                slot,
                {"head": flip(head, 2 << j)},
            )
            copy.start()
            flight.append((copy, base + bit * (1 << j), slot))
        return flight, part, got, first, count

    def finish(state):
        flight, (start, size), got, first, count = state
        for copy, keep, slot in flight:
            copy.wait()

            def add(m, carry, keep=keep, slot=slot):
                acc[keep, first + m, start : start + size] += got[slot, m]
                return carry

            lax.fori_loop(0, count, add, 0)

    own = dp * share
    for step in range(bits):
        if step:
            state_a = begin(part_a, got_a, sem_a, up, step, 0, per_head)
            state_b = begin(part_b, got_b, sem_b, down, step, 0, per_head)
        else:
            state_a = early["a"], part_a, got_a, 0, per_head
            state_b = early["b"], part_b, got_b, 0, per_head
        finish(state_a)
        finish(state_b)
    rows_ab = pl.ds(0, part_c[0])
    flight_y = []
    for o, peer in enumerate(peers):
        copy = remote(acc.at[mine, pl.ds(peer * share, share), rows_ab], got_y.at[o], sem_y, o, {"dp": peer})
        copy.start()
        flight_y.append(copy)
    for copy in flight_z:
        copy.wait()
    for e in range(chunks):

        def add_z(m, carry, c=chunk_of(e), e=e):
            value = acc[c, own + m, part_c[0] :]
            for o in range(len(peers)):
                value += got_z[o, e, m]
            acc[c, own + m, part_c[0] :] = value
            return carry

        lax.fori_loop(0, share, add_z, 0)
    for step in range(bits):
        finish(begin(part_c, got_c, sem_c, up, step, own, share))
    for copy in flight_y:
        copy.wait()

    def add_y(m, carry):
        value = acc[mine, own + m, : part_c[0]]
        for o in range(len(peers)):
            value += got_y[o, m]
        out_ref[m, : part_c[0]] = value
        out_ref[m, part_c[0] :] = acc[mine, own + m, part_c[0] :]
        return carry

    lax.fori_loop(0, share, add_y, 0)


def gram_sums(projected, weights, n_head, n_dp):
    tokens, width = projected.shape
    mats, rows, lanes = width // HD, HD, 2 * BLK
    per_head = mats // n_head
    share = per_head // n_dp
    chunks = n_head // 2
    (_, rows_a), (_, rows_b), (_, rows_c) = part_rows()
    f32 = jnp.float32
    return pl.pallas_call(
        functools.partial(scatter_kernel, n_head, n_dp, share),
        in_specs=[pl.BlockSpec(memory_space=pl.ANY), pl.BlockSpec(memory_space=pltpu.VMEM)],
        out_specs=pl.BlockSpec(memory_space=pltpu.VMEM),
        out_shape=jax.ShapeDtypeStruct((share, rows, lanes), f32),
        scratch_shapes=[
            pltpu.VMEM((chunks, per_head, rows, lanes), f32),
            pltpu.VMEM((chunks, per_head, rows, lanes), f32),
            pltpu.VMEM((per_head, rows, lanes), f32),
            pltpu.VMEM((tokens, 2 * HD), projected.dtype),
            pltpu.VMEM((2, tokens, per_head * HD), projected.dtype),
            pltpu.VMEM((chunks - 1, per_head, rows_a, lanes), f32),
            pltpu.VMEM((chunks - 1, per_head, rows_b, lanes), f32),
            pltpu.VMEM((chunks - 1, share, rows_c, lanes), f32),
            pltpu.VMEM((n_dp - 1, chunks, share, rows_c, lanes), f32),
            pltpu.VMEM((n_dp - 1, share, rows - rows_c, lanes), f32),
            pltpu.SemaphoreType.DMA((2,)),
            pltpu.SemaphoreType.DMA((2, chunks)),
            pltpu.SemaphoreType.DMA((2, chunks - 1)),
            pltpu.SemaphoreType.DMA((2, chunks - 1)),
            pltpu.SemaphoreType.DMA((2, chunks - 1)),
            pltpu.SemaphoreType.DMA((2, (n_dp - 1) * chunks)),
            pltpu.SemaphoreType.DMA((2, n_dp - 1)),
        ],
        compiler_params=pltpu.CompilerParams(collective_id=0, has_side_effects=True, vmem_limit_bytes=60 << 20),
    )(projected, weights)


def gather_kernel(n_dp, share, packed_ref, out_ref, got, sems):
    dp = lax.axis_index("dp")
    peers = [lax.rem(dp + o, n_dp) for o in range(1, n_dp)]
    greet([], peers)
    flight = []
    for o, peer in enumerate(peers):
        copy = remote(packed_ref, got.at[o], sems, o, {"dp": peer})
        copy.start()
        flight.append(copy)
    two = 2 * BLK

    def unpack(source, base):
        def one(m, carry):
            top = source[m, :BLK]
            out_ref[base + m, :BLK, :two] = jnp.where(lax.broadcasted_iota(jnp.int32, (BLK, two), 1) < BLK, top, 0.0)
            out_ref[base + m, BLK:, :two] = source[m, BLK:]
            out_ref[base + m, :two, two:] = jnp.zeros((two, BLK), jnp.float32)
            out_ref[base + m, two:, two:] = top[:, BLK:]
            return carry

        lax.fori_loop(0, share, one, 0)

    unpack(packed_ref, dp * share)
    for o in range(n_dp - 1):
        flight[o].wait()
        unpack(got.at[o], lax.rem(dp + n_dp - 1 - o, n_dp) * share)


def gather(packed, n_dp):
    share, rows, lanes = packed.shape
    return pl.pallas_call(
        functools.partial(gather_kernel, n_dp, share),
        in_specs=[pl.BlockSpec(memory_space=pltpu.VMEM)],
        out_specs=pl.BlockSpec(memory_space=pltpu.VMEM),
        out_shape=jax.ShapeDtypeStruct((n_dp * share, HD, HD), jnp.float32),
        scratch_shapes=[
            pltpu.VMEM((n_dp - 1, share, rows, lanes), jnp.float32),
            pltpu.SemaphoreType.DMA((2, n_dp - 1)),
        ],
        compiler_params=pltpu.CompilerParams(collective_id=1, has_side_effects=True),
    )(packed)


def on_device(projected, weight_exp, damp_exp):
    n_head = lax.axis_size("head")
    n_dp = lax.axis_size("dp")
    mats = projected.shape[1] // HD
    share = mats // (n_head * n_dp)
    total = projected.shape[0] * n_head * n_dp
    weights = jnp.exp2(weight_exp.astype(jnp.float32)).astype(jnp.bfloat16)
    owned = gram_sums(projected, weights[:, None], n_head, n_dp)
    first = (lax.axis_index("head") * n_dp + lax.axis_index("dp")) * share
    damp = jnp.exp2(-lax.dynamic_slice_in_dim(damp_exp, first, share, 0).astype(jnp.float32))
    factors = whiten(owned, damp, float(total))
    return gather(factors, n_dp)


def solution(mesh):
    return jax.shard_map(
        on_device,
        mesh=mesh,
        in_specs=(P(("dp", "head"), None), P(("dp", "head")), P()),
        out_specs=P("head", None, None),
        check_vma=False,
    )
```

profile of v0, /device:TPU:24, one launch (start us, length us, event | category | flops | bytes accessed | tf_op | source)
XLA Modules:
  0.0 151.4 jit_solution(17621260722162096797)
XLA Ops:
  0.0 1.3 multiply_exponential_fusion.damp_ref
  1.3 0.7 exponential_convert_fusion
  2.0 0.8 broadcast_in_dim.4.weights_ref
  2.8 79.6 %shard_map.37.packed_ref = f32[4,192,128]{2,1,0:T(8,128)} custom-call(bf16[384,24576]{1,0:T(8,128)(2,1)} %rows_ref.1, bf16[384,1]{1,0:T(8,128)(2,1)} %broadcast_in_dim.4.weights_ref), custom_call_target="tpu_custom_call" | custom-call | tf_op jit(solution)/shard_map/pallas_call | solution.py:330
  82.4 25.9 %shard_map.38.packed_ref = f32[4,192,128]{2,1,0:T(8,128)} custom-call(f32[4]{0:T(128)} %multiply_exponential_fusion.damp_ref, f32[4,192,128]{2,1,0:T(8,128)} %shard_map.37.packed_ref), custom_call_target="tpu_custom_call" | custom-call | tf_op jit(solution)/shard_map/pallas_call | solution.py:125
  108.3 39.2 %shard_map.39 = f32[16,192,192]{2,1,0:T(8,128)} custom-call(f32[4,192,128]{2,1,0:T(8,128)} %shard_map.38.packed_ref), custom_call_target="tpu_custom_call" | custom-call | tf_op jit(solution)/shard_map/pallas_call | solution.py:388
  147.5 3.8 %copy.6 = f32[16,192,192]{2,1,0:T(8,128)} copy(f32[16,192,192]{2,1,0:T(8,128)} %shard_map.39) | data formatting | bytes 4718592
where the time goes:
time: 152 us; the launch traced here: 151 us
  Pallas kernels  145 us (95%)
  local copies, waits for them, and re-layouts  4.6 us (3%)
  other arithmetic  2 us (1%)
    pallas_call x1, Pallas kernels, gram_sums(): pl.pallas_call(functools.partial(scatter_kernel, n_head, n_dp, share), in...  79.6 us
    pallas_call x1, Pallas kernels, gather(): pl.pallas_call(functools.partial(gather_kernel, n_dp, share), in_specs=[p...  39.2 us
    pallas_call x1, Pallas kernels, whiten(): pl.pallas_call(functools.partial(whiten_kernel, total, count), in_specs=[...  25.9 us
    unnamed x1, local copies, waits for them, and re-layouts  3.83 us

commit v1 on v0

--- a/solution.py
+++ b/solution.py
@@ -10,6 +10,8 @@
 HD = 192
 BLK = HD // 3
 HIGH = lax.Precision.HIGHEST
+LEVELS = 32767.0
+TINY = 1e-30
 
 
 def store_pair(rows, wide, out, at):
@@ -82,7 +84,15 @@
     return got[two:, :BLK], got[BLK:two, :BLK], got[two:, BLK:], got[:BLK, :].T, got[BLK:two, BLK:].T
 
 
-def whiten_kernel(total, count, damp_ref, packed_ref, out_ref):
+def encode(value, scale):
+    return jnp.round(value * scale).astype(jnp.int32).astype(jnp.int16)
+
+
+def decode(code):
+    return code.astype(jnp.int32).astype(jnp.float32)
+
+
+def whiten_kernel(total, count, damp_ref, packed_ref, out_ref, step_ref):
     two = 2 * BLK
     diag = lax.broadcasted_iota(jnp.int32, (BLK, BLK), 0) == lax.broadcasted_iota(jnp.int32, (BLK, BLK), 1)
     a11, a22, a33, low, a32 = [], [], [], [], []
@@ -115,9 +125,13 @@
         w21 = -dot(w22[m], below[:BLK])
         w32 = -dot(w33[m], dot(l32[m], w22[m]))
         w31 = -dot(w33[m], below[BLK:] + dot(l32[m], w21))
-        out_ref[m, :BLK] = jnp.concatenate((w11[m], w33[m]), axis=1)
-        out_ref[m, BLK:two] = jnp.concatenate((w21, w22[m]), axis=1)
-        out_ref[m, two:] = jnp.concatenate((w31, w32), axis=1)
+        bands = ((w11[m], w33[m]), (w21, w22[m]), (w31, w32))
+        bands = [jnp.concatenate(band, axis=1) for band in bands]
+        top = functools.reduce(jnp.maximum, [jnp.max(jnp.abs(band), axis=0, keepdims=True) for band in bands])
+        top = jnp.maximum(top, TINY)
+        step_ref[m] = top / LEVELS
+        for n, band in enumerate(bands):
+            out_ref[m, n * BLK : (n + 1) * BLK] = encode(band, LEVELS / top)
 
 
 def whiten(packed, damp, total):
@@ -125,8 +139,11 @@
     return pl.pallas_call(
         functools.partial(whiten_kernel, total, count),
         in_specs=[pl.BlockSpec(memory_space=pltpu.SMEM), pl.BlockSpec(memory_space=pltpu.VMEM)],
-        out_specs=pl.BlockSpec(memory_space=pltpu.VMEM),
-        out_shape=jax.ShapeDtypeStruct(packed.shape, jnp.float32),
+        out_specs=[pl.BlockSpec(memory_space=pltpu.VMEM)] * 2,
+        out_shape=[
+            jax.ShapeDtypeStruct(packed.shape, jnp.int16),
+            jax.ShapeDtypeStruct((count, 1, packed.shape[2]), jnp.float32),
+        ],
     )(damp, packed)
 
 
@@ -355,47 +372,71 @@
     )(projected, weights)
 
 
-def gather_kernel(n_dp, share, packed_ref, out_ref, got, sems):
+def gather_kernel(n_dp, share, code_ref, step_ref, codes, steps, sems, step_sems, own_sems):
     dp = lax.axis_index("dp")
     peers = [lax.rem(dp + o, n_dp) for o in range(1, n_dp)]
+    mine = pl.ds(dp * share, share)
+    own = [
+        pltpu.make_async_copy(code_ref, codes.at[mine], own_sems.at[0]),
+        pltpu.make_async_copy(step_ref, steps.at[mine], own_sems.at[1]),
+    ]
+    for copy in own:
+        copy.start()
     greet([], peers)
     flight = []
     for o, peer in enumerate(peers):
-        copy = remote(packed_ref, got.at[o], sems, o, {"dp": peer})
+        flight.append(remote(code_ref, codes.at[mine], sems, o, {"dp": peer}))
+        flight.append(remote(step_ref, steps.at[mine], step_sems, o, {"dp": peer}))
+    for copy in flight:
         copy.start()
-        flight.append(copy)
-    two = 2 * BLK
-
-    def unpack(source, base):
-        def one(m, carry):
-            top = source[m, :BLK]
-            out_ref[base + m, :BLK, :two] = jnp.where(lax.broadcasted_iota(jnp.int32, (BLK, two), 1) < BLK, top, 0.0)
-            out_ref[base + m, BLK:, :two] = source[m, BLK:]
-            out_ref[base + m, :two, two:] = jnp.zeros((two, BLK), jnp.float32)
-            out_ref[base + m, two:, two:] = top[:, BLK:]
-            return carry
-
-        lax.fori_loop(0, share, one, 0)
-
-    unpack(packed_ref, dp * share)
-    for o in range(n_dp - 1):
-        flight[o].wait()
-        unpack(got.at[o], lax.rem(dp + n_dp - 1 - o, n_dp) * share)
-
-
-def gather(packed, n_dp):
-    share, rows, lanes = packed.shape
+    for copy in own + flight:
+        copy.wait()
+
+
+def gather(code, step, n_dp):
+    share = code.shape[0]
     return pl.pallas_call(
         functools.partial(gather_kernel, n_dp, share),
-        in_specs=[pl.BlockSpec(memory_space=pltpu.VMEM)],
-        out_specs=pl.BlockSpec(memory_space=pltpu.VMEM),
-        out_shape=jax.ShapeDtypeStruct((n_dp * share, HD, HD), jnp.float32),
+        in_specs=[pl.BlockSpec(memory_space=pltpu.VMEM)] * 2,
+        out_specs=[pl.BlockSpec(memory_space=pltpu.VMEM)] * 2,
+        out_shape=[
+            jax.ShapeDtypeStruct((n_dp * share, *code.shape[1:]), code.dtype),
+            jax.ShapeDtypeStruct((n_dp * share, *step.shape[1:]), step.dtype),
+        ],
         scratch_shapes=[
-            pltpu.VMEM((n_dp - 1, share, rows, lanes), jnp.float32),
             pltpu.SemaphoreType.DMA((2, n_dp - 1)),
+            pltpu.SemaphoreType.DMA((2, n_dp - 1)),
+            pltpu.SemaphoreType.DMA((2,)),
         ],
         compiler_params=pltpu.CompilerParams(collective_id=1, has_side_effects=True),
-    )(packed)
+    )(code, step)
+
+
+def unpack_kernel(code_ref, step_ref, out_ref):
+    two = 2 * BLK
+    left = lax.broadcasted_iota(jnp.int32, (BLK, two), 1) < BLK
+    for m in range(out_ref.shape[0]):
+        step = step_ref[m]
+        top = decode(code_ref[m, :BLK]) * step
+        out_ref[m, :BLK, :two] = jnp.where(left, top, 0.0)
+        out_ref[m, BLK:, :two] = decode(code_ref[m, BLK:]) * step
+        out_ref[m, :two, two:] = jnp.zeros((two, BLK), jnp.float32)
+        out_ref[m, two:, two:] = top[:, BLK:]
+
+
+def unpack(codes, steps):
+    mats, rows, lanes = codes.shape
+    group = 2
+    return pl.pallas_call(
+        unpack_kernel,
+        grid=(mats // group,),
+        in_specs=[
+            pl.BlockSpec((group, rows, lanes), lambda i: (i, 0, 0)),
+            pl.BlockSpec((group, 1, lanes), lambda i: (i, 0, 0)),
+        ],
+        out_specs=pl.BlockSpec((group, HD, HD), lambda i: (i, 0, 0)),
+        out_shape=jax.ShapeDtypeStruct((mats, HD, HD), jnp.float32),
+    )(codes, steps)
 
 
 def on_device(projected, weight_exp, damp_exp):
@@ -408,8 +449,9 @@
     owned = gram_sums(projected, weights[:, None], n_head, n_dp)
     first = (lax.axis_index("head") * n_dp + lax.axis_index("dp")) * share
     damp = jnp.exp2(-lax.dynamic_slice_in_dim(damp_exp, first, share, 0).astype(jnp.float32))
-    factors = whiten(owned, damp, float(total))
-    return gather(factors, n_dp)
+    code, step = whiten(owned, damp, float(total))
+    codes, steps = gather(code, step, n_dp)
+    return unpack(codes, steps)
 
 
 def solution(mesh):

time: 152 us -> 136 us (0.89)
  Pallas kernels: 145 us -> 133 us
  local copies, waits for them, and re-layouts: 4.6 us -> 0.77 us
    pallas_call x1, Pallas kernels: 39.2 us -> 21.3 us  [gather(): pl.pallas_call(functools.partial(gather_kernel, n_dp, share), in_specs=[p...]
    pallas_call x0 -> x1, Pallas kernels: none -> 5.79 us  [unpack(): pl.pallas_call(unpack_kernel, grid=(mats // group,), in_specs=[pl.BlockSp...]
    unnamed x1 -> x0, local copies, waits for them, and re-layouts: 3.83 us -> none
where the time goes in v1:
time: 136 us; the launch traced here: 135 us
  Pallas kernels  133 us (98%)
  other arithmetic  2.01 us (1%)
    pallas_call x1, Pallas kernels, gram_sums(): pl.pallas_call(functools.partial(scatter_kernel, n_head, n_dp, share), in...  79.6 us
    pallas_call x1, Pallas kernels, whiten(): pl.pallas_call(functools.partial(whiten_kernel, total, count), in_specs=[...  25.9 us
    pallas_call x1, Pallas kernels, gather(): pl.pallas_call(functools.partial(gather_kernel, n_dp, share), in_specs=[p...  21.3 us
    pallas_call x1, Pallas kernels, unpack(): pl.pallas_call(unpack_kernel, grid=(mats // group,), in_specs=[pl.BlockSp...  5.79 us

profile of v1, /device:TPU:24, one launch (start us, length us, event | category | flops | bytes accessed | tf_op | source)
XLA Modules:
  0.0 135.5 jit_solution(2781039068451582897)
XLA Ops:
  0.0 1.3 multiply_exponential_fusion.damp_ref
  1.3 0.7 exponential_convert_fusion
  2.0 0.8 broadcast_in_dim.4.weights_ref
  2.8 79.6 %shard_map.37.packed_ref = f32[4,192,128]{2,1,0:T(8,128)} custom-call(bf16[384,24576]{1,0:T(8,128)(2,1)} %rows_ref.1, bf16[384,1]{1,0:T(8,128)(2,1)} %broadcast_in_dim.4.weights_ref), custom_call_target="tpu_custom_call" | custom-call | tf_op jit(solution)/shard_map/pallas_call | solution.py:347
  82.4 25.9 %shard_map.38 = (s16[4,192,128]{2,1,0:T(8,128)(2,1)}, f32[4,1,128]{2,1,0:T(1,128)}) custom-call(f32[4]{0:T(128)} %multiply_exponential_fusion.damp_ref, f32[4,192,128]{2,1,0:T(8,128)} %shard_map.37.packed_ref), custom_call_target="tpu_custom_call" | custom-call | tf_op jit(solution)/shard_map/pallas_call | solution.py:139
  108.3 21.3 %shard_map.39 = (s16[16,192,128]{2,1,0:T(8,128)(2,1)}, f32[16,1,128]{2,1,0:T(1,128)}) custom-call(s16[4,192,128]{2,1,0:T(8,128)(2,1)} %get-tuple-element.9.code_ref, f32[4,1,128]{2,1,0:T(1,128)} %get-tuple-element.10.step_ref), custom_call_target="tpu_custom_call" | custom-call | tf_op jit(solution)/shard_map/pallas_call | solution.py:398
  129.7 5.8 %shard_map.40 = f32[16,192,192]{2,1,0:T(8,128)} custom-call(s16[16,192,128]{2,1,0:T(8,128)(2,1)} %get-tuple-element.11.code_ref, f32[16,1,128]{2,1,0:T(1,128)} %get-tuple-element.12.step_ref), custom_call_target="tpu_custom_call" | custom-call | tf_op jit(solution)/shard_map/pallas_call | solution.py:430

commit v2 on v1

--- a/solution.py
+++ b/solution.py
@@ -1,4 +1,5 @@
 import functools
+import math
 
 import jax
 import jax.numpy as jnp
@@ -12,6 +13,8 @@
 HIGH = lax.Precision.HIGHEST
 LEVELS = 32767.0
 TINY = 1e-30
+DEPTH = 4
+LAG = 3
 
 
 def store_pair(rows, wide, out, at):
@@ -171,13 +174,60 @@
     pl.semaphore_wait(barrier, len(heads) + len(dps))
 
 
-def part_rows():
-    last = HD // 4
-    first = (HD - last) // 2
-    return (0, first), (first, first), (2 * first, last)
-
-
-def scatter_kernel(n_head, n_dp, share, rows_ref, weights_ref, out_ref, acc, sent, own_grams, wide, columns, got_a, got_b, got_c, got_z, got_y, sem_in, sem_0, sem_a, sem_b, sem_c, sem_z, sem_y):
+def outer_steps(t, u, odd):
+    shape = (8, 2 * BLK)
+    low = lax.broadcasted_iota(jnp.int32, shape, 1) < BLK
+    sub = lax.broadcasted_iota(jnp.int32, shape, 0)
+    t, u = jnp.broadcast_to(t, shape), jnp.broadcast_to(u, shape)
+    turned_t, turned_u = pltpu.roll(t, BLK, 1), pltpu.roll(u, BLK, 1)
+    down = jnp.where(low, t, turned_u) if odd else jnp.where(low, turned_u, t)
+    across = jnp.where(low, u, t) if odd else jnp.where(low, t, u)
+    wide = jnp.where(sub == 0, down, 0.0)
+    corner = jnp.where(sub == 1, t, jnp.where(sub == 2, turned_t, 0.0))
+    left = jnp.concatenate((wide, corner[:, :BLK]), axis=1).astype(jnp.bfloat16)
+    third = jnp.where((sub == 2) & ~low, t, 0.0)
+    right = jnp.where(sub == 0, across, jnp.where((sub == 1) & low, t, third)).astype(jnp.bfloat16)
+    grid = lax.dot_general(left, right, (((0,), (0,)), ((), ())), preferred_element_type=jnp.float32)
+    if odd:
+        return grid
+    return jnp.concatenate((grid[2 * BLK :], grid[: 2 * BLK]), axis=0)
+
+
+def column_steps(value, odd):
+    two = 2 * BLK
+    lane = lax.broadcasted_iota(jnp.int32, (BLK, two), 1)
+    hit = lane % BLK == lax.broadcasted_iota(jnp.int32, (BLK, two), 0)
+    corner, middle = (value[two:], value[BLK:two]) if odd else (value[:BLK], value[BLK:two])
+    near = lane < BLK if odd else lane >= BLK
+    t = jnp.sum(jnp.where(hit, corner, 0.0), axis=0, keepdims=True)
+    u = jnp.sum(jnp.where(hit & near, middle, 0.0), axis=0, keepdims=True)
+    scale = (1.0 + 2.0**-8) / math.sqrt(LEVELS - 1.0)
+    t, u = (jnp.sqrt(jnp.maximum(d, TINY)) * scale for d in (t, u))
+    return tuple(s.astype(jnp.bfloat16).astype(jnp.float32) for s in (t, u))
+
+
+def put_code(value, odd, code, step, slot, m):
+    t, u = column_steps(value, odd)
+    step[slot, m, 0:1] = t
+    step[slot, m, 1:2] = u
+    code[slot, m] = jnp.round(value / outer_steps(t, u, odd)).astype(jnp.int32).astype(jnp.int16)
+
+
+def get_code(odd, code, step, slot, m):
+    return decode(code[slot, m]) * outer_steps(step[slot, m, 0:1], step[slot, m, 1:2], odd)
+
+
+def get_code_either(odd, code, step, slot, m):
+    if isinstance(odd, int):
+        return get_code(odd, code, step, slot, m)
+    return jnp.where(odd == 1, get_code(1, code, step, slot, m), get_code(0, code, step, slot, m))
+
+
+def first_step(e, order):
+    return next((s for s, j in enumerate(order) if (e >> j) & 1), len(order))
+
+
+def scatter_kernel(n_head, n_dp, share, waves, rows_ref, weights_ref, out_ref, acc, half, sent, wide, columns, code_out, code_in, step_out, step_in, far_out, far_in, far_step_out, far_step_in, sem_in, sem_0, sem_code, sem_step, sem_far, sem_far_step):
     head = lax.axis_index("head")
     dp = lax.axis_index("dp")
     chunks = n_head // 2
@@ -185,12 +235,12 @@
     mine = head // 2
     core = head % 2
     per_head = share * n_dp
-    span = per_head * HD
+    mats = per_head // waves
+    span = mats * HD
+    owners = n_dp // waves
+    place = lax.rem(dp, owners)
     peers = [lax.rem(dp + o, n_dp) for o in range(1, n_dp)]
-    part_a, part_b, part_c = part_rows()
-    up = list(range(bits))
-    down = up[::-1]
-    rows_c = pl.ds(part_c[0], part_c[1])
+    orders = list(range(bits)), list(range(bits))[::-1]
 
     def chunk_of(e):
         chunk = mine
@@ -199,141 +249,139 @@
                 chunk = chunk + (1 - 2 * ((mine // (1 << j)) % 2)) * (1 << j)
         return chunk
 
-    order = list(range(chunks))[::-1]
+    groups = [lax.rem(dp // owners + 1 + w, waves) for w in range(waves)]
+    tasks = [(w, e) for w in range(waves) for e in range(chunks)[::-1]]
     visits = []
-    for e in order:
-        visits += [2 * chunk_of(e) + 1 - core, 2 * chunk_of(e) + core]
+    for w, e in tasks:
+        for side in (1 - core, core):
+            visits.append((2 * chunk_of(e) + side) * per_head + groups[w] * mats)
 
     def fetch(v):
-        start = pl.multiple_of(visits[v] * span, 2 * BLK)
-        return pltpu.make_async_copy(rows_ref.at[:, pl.ds(start, span)], columns.at[v % 2], sem_in.at[v % 2])
-
-    fetch(0).start()
+        start = pl.multiple_of(visits[v] * HD, 2 * BLK)
+        slot = v % DEPTH
+        return pltpu.make_async_copy(rows_ref.at[:, pl.ds(start, span)], columns.at[slot], sem_in.at[slot])
+
+    for v in range(DEPTH - 1):
+        fetch(v).start()
     wide[...] = jnp.broadcast_to(weights_ref[...], wide.shape)
     greet([flip(head, 1 << j) for j in range(bits + 1)], peers)
 
     def multiply(v, out):
-        if v + 1 < len(visits):
-            fetch(v + 1).start()
+        if v + DEPTH - 1 < len(visits):
+            fetch(v + DEPTH - 1).start()
         fetch(v).wait()
 
         def pair(i, carry):
             start = pl.multiple_of(i * 2 * HD, 2 * BLK)
-            store_pair(columns[v % 2, :, pl.ds(start, 2 * HD)], wide[...], out, 2 * i)
+            store_pair(columns[v % DEPTH, :, pl.ds(start, 2 * HD)], wide[...], out, 2 * i)
             return carry
 
-        lax.fori_loop(0, per_head // 2, pair, 0, unroll=2)
-
-    def squeeze(e, j):
-        return (e >> (j + 1) << j) | (e & ((1 << j) - 1))
-
-    early = {"a": [], "b": []}
-    flight_z = []
-    for n, e in enumerate(order):
-        c = chunk_of(e)
-        multiply(2 * n, sent.at[n])
-        copy = remote(sent.at[n], acc.at[c], sem_0, n, {"head": flip(head, 1)})
-        copy.start()
-        multiply(2 * n + 1, own_grams)
+        lax.fori_loop(0, mats // 2, pair, 0, unroll=True)
+
+    def swap(k):
+        return remote(sent.at[k], half.at[k], sem_0, k, {"head": flip(head, 1)})
+
+    def near_slot(w, e, odd):
+        return (w * (chunks - 1) + e - 1) * 2 + odd
+
+    def pass_on(w, e, odd):
+        slot = near_slot(w, e, odd)
+        peer = {"head": flip(head, 2 << orders[odd][first_step(e, orders[odd])])}
+        return [
+            remote(code_out.at[slot], code_in.at[slot], sem_code, slot, peer),
+            remote(step_out.at[slot], step_in.at[slot], sem_step, slot, peer),
+        ]
+
+    def receipts(e, odd):
+        order = orders[odd]
+        return [e | (1 << order[s]) for s in range(first_step(e, order))]
+
+    def merge(k, odd):
+        w, e = tasks[k]
+        got = [near_slot(w, other, odd) for other in receipts(e, odd)]
+        for other in receipts(e, odd):
+            for copy in pass_on(w, other, odd):
+                copy.wait()
+
+        def one(i, carry):
+            m = 2 * i + odd
+            value = acc[k, m] + half[k, m]
+            for slot in got:
+                value += get_code(odd, code_in, step_in, slot, i)
+            if e:
+                put_code(value, odd, code_out, step_out, near_slot(w, e, odd), i)
+            else:
+                if w == waves - 1:
+                    acc[k, m] = value
+                if w < waves - 1 or owners > 1:
+                    put_code(value, odd, far_out, far_step_out, w, m)
+            return carry
+
+        lax.fori_loop(0, mats // 2, one, 0, unroll=True)
+        if e:
+            for copy in pass_on(w, e, odd):
+                copy.start()
+
+    def send_far(w):
+        flight = []
+        for turn in range(w == waves - 1, owners):
+            owner = lax.rem(place + turn, owners)
+            slot = w * owners + (owners - turn) % owners
+            part = pl.ds(owner * share, share)
+            peer = {"dp": groups[w] * owners + owner}
+            flight.append((remote(far_out.at[w, part], far_in.at[slot], sem_far, slot, peer), slot))
+            flight.append((remote(far_step_out.at[w, part], far_step_in.at[slot], sem_far_step, slot, peer), slot))
+        for copy, _ in flight:
+            copy.start()
+        return flight
+
+    plan = {}
+    for k, (w, e) in enumerate(tasks):
+        for odd in (0, 1):
+            waits = len(receipts(e, odd))
+            at = k + 1 if not waits else k + LAG * waits
+            plan.setdefault(at, []).append((k, odd))
+    swapped = set()
+    far = []
+    for t in range(max(len(tasks), max(plan) + 1)):
+        for k, odd in plan.get(t, ()):
+            if k not in swapped:
+                swap(k).wait()
+                swapped.add(k)
+            merge(k, odd)
+        for k in sorted({k for k, odd in plan.get(t, ()) if tasks[k][1] == 0}):
+            far += send_far(tasks[k][0])
+        if t < len(tasks):
+            multiply(2 * t, sent.at[t])
+            swap(t).start()
+            multiply(2 * t + 1, acc.at[t])
+    for copy, _ in far:
         copy.wait()
-
-        def add(m, carry, c=c):
-            acc[c, m] += own_grams[m]
-            return carry
-
-        lax.fori_loop(0, per_head, add, 0)
-        for name, (start, size), got, sems, j in (("a", part_a, got_a, sem_a, up[0]), ("b", part_b, got_b, sem_b, down[0])):
-            if (e >> j) & 1:
-                slot = squeeze(e, j)
-                out = remote(
-                    acc.at[c, pl.ds(0, per_head), pl.ds(start, size)], got.at[slot], sems, slot, {"head": flip(head, 2 << j)}
-                )
-                out.start()
-                early[name].append((out, chunk_of(e ^ (1 << j)), slot))
-        for o, peer in enumerate(peers):
-            out = remote(
-                acc.at[c, pl.ds(peer * share, share), rows_c], got_z.at[o, e], sem_z, o * chunks + e, {"dp": peer}
-            )
-            out.start()
-            flight_z.append(out)
-
-    def begin(part, got, sems, order, step, first, count):
-        j = order[step]
-        bit = (mine // (1 << j)) % 2
-        fixed = 0
-        for done in order[:step]:
-            fixed = fixed + (mine // (1 << done)) % 2 * (1 << done)
-        free = [b for b in range(bits) if b not in order[: step + 1]]
-        flight = []
-        start, size = part
-        offset = sum(chunks >> (s + 1) for s in range(step))
-        for e in range(1 << len(free)):
-            base = fixed + sum(((e >> i) & 1) << b for i, b in enumerate(free))
-            slot = offset + e
-            copy = remote(
-                acc.at[base + (1 - bit) * (1 << j), pl.ds(first, count), pl.ds(start, size)],
-                got.at[slot],
-                sems,
-                slot,
-                {"head": flip(head, 2 << j)},
-            )
-            copy.start()
-            flight.append((copy, base + bit * (1 << j), slot))
-        return flight, part, got, first, count
-
-    def finish(state):
-        flight, (start, size), got, first, count = state
-        for copy, keep, slot in flight:
-            copy.wait()
-
-            def add(m, carry, keep=keep, slot=slot):
-                acc[keep, first + m, start : start + size] += got[slot, m]
-                return carry
-
-            lax.fori_loop(0, count, add, 0)
-
-    own = dp * share
-    for step in range(bits):
-        if step:
-            state_a = begin(part_a, got_a, sem_a, up, step, 0, per_head)
-            state_b = begin(part_b, got_b, sem_b, down, step, 0, per_head)
-        else:
-            state_a = early["a"], part_a, got_a, 0, per_head
-            state_b = early["b"], part_b, got_b, 0, per_head
-        finish(state_a)
-        finish(state_b)
-    rows_ab = pl.ds(0, part_c[0])
-    flight_y = []
-    for o, peer in enumerate(peers):
-        copy = remote(acc.at[mine, pl.ds(peer * share, share), rows_ab], got_y.at[o], sem_y, o, {"dp": peer})
-        copy.start()
-        flight_y.append(copy)
-    for copy in flight_z:
-        copy.wait()
-    for e in range(chunks):
-
-        def add_z(m, carry, c=chunk_of(e), e=e):
-            value = acc[c, own + m, part_c[0] :]
-            for o in range(len(peers)):
-                value += got_z[o, e, m]
-            acc[c, own + m, part_c[0] :] = value
-            return carry
-
-        lax.fori_loop(0, share, add_z, 0)
-    for step in range(bits):
-        finish(begin(part_c, got_c, sem_c, up, step, own, share))
-    for copy in flight_y:
-        copy.wait()
-
-    def add_y(m, carry):
-        value = acc[mine, own + m, : part_c[0]]
-        for o in range(len(peers)):
-            value += got_y[o, m]
-        out_ref[m, : part_c[0]] = value
-        out_ref[m, part_c[0] :] = acc[mine, own + m, part_c[0] :]
+    slots = sorted({slot for _, slot in far})
+    last = len(tasks) - 1
+
+    def total(m, carry, odd):
+        value = acc[last, place * share + m]
+        for slot in slots:
+            value += get_code_either(odd, far_in, far_step_in, slot, m)
+        out_ref[m] = value
         return carry
 
-    lax.fori_loop(0, share, add_y, 0)
+    if share % 2:
+        lax.fori_loop(0, share, lambda m, c: total(m, c, lax.rem(place * share + m, 2)), 0)
+    else:
+
+        def both(i, carry):
+            return total(2 * i + 1, total(2 * i, carry, 0), 1)
+
+        lax.fori_loop(0, share // 2, both, 0, unroll=True)
+
+
+def wave_count(per_head, n_dp):
+    waves = n_dp
+    while waves > 1 and (per_head % waves or (per_head // waves) % 2 or n_dp % waves):
+        waves -= 1
+    return waves
 
 
 def gram_sums(projected, weights, n_head, n_dp):
@@ -342,31 +390,36 @@
     per_head = mats // n_head
     share = per_head // n_dp
     chunks = n_head // 2
-    (_, rows_a), (_, rows_b), (_, rows_c) = part_rows()
-    f32 = jnp.float32
+    waves = wave_count(per_head, n_dp)
+    group = per_head // waves
+    tasks = waves * chunks
+    near = 2 * waves * (chunks - 1)
+    f32, i16 = jnp.float32, jnp.int16
     return pl.pallas_call(
-        functools.partial(scatter_kernel, n_head, n_dp, share),
+        functools.partial(scatter_kernel, n_head, n_dp, share, waves),
         in_specs=[pl.BlockSpec(memory_space=pl.ANY), pl.BlockSpec(memory_space=pltpu.VMEM)],
         out_specs=pl.BlockSpec(memory_space=pltpu.VMEM),
         out_shape=jax.ShapeDtypeStruct((share, rows, lanes), f32),
         scratch_shapes=[
-            pltpu.VMEM((chunks, per_head, rows, lanes), f32),
-            pltpu.VMEM((chunks, per_head, rows, lanes), f32),
-            pltpu.VMEM((per_head, rows, lanes), f32),
+            pltpu.VMEM((tasks, group, rows, lanes), f32),
+            pltpu.VMEM((tasks, group, rows, lanes), f32),
+            pltpu.VMEM((tasks, group, rows, lanes), f32),
             pltpu.VMEM((tokens, 2 * HD), projected.dtype),
-            pltpu.VMEM((2, tokens, per_head * HD), projected.dtype),
-            pltpu.VMEM((chunks - 1, per_head, rows_a, lanes), f32),
-            pltpu.VMEM((chunks - 1, per_head, rows_b, lanes), f32),
-            pltpu.VMEM((chunks - 1, share, rows_c, lanes), f32),
-            pltpu.VMEM((n_dp - 1, chunks, share, rows_c, lanes), f32),
-            pltpu.VMEM((n_dp - 1, share, rows - rows_c, lanes), f32),
-            pltpu.SemaphoreType.DMA((2,)),
-            pltpu.SemaphoreType.DMA((2, chunks)),
-            pltpu.SemaphoreType.DMA((2, chunks - 1)),
-            pltpu.SemaphoreType.DMA((2, chunks - 1)),
-            pltpu.SemaphoreType.DMA((2, chunks - 1)),
-            pltpu.SemaphoreType.DMA((2, (n_dp - 1) * chunks)),
-            pltpu.SemaphoreType.DMA((2, n_dp - 1)),
+            pltpu.VMEM((DEPTH, tokens, group * HD), projected.dtype),
+            pltpu.VMEM((near, group // 2, rows, lanes), i16),
+            pltpu.VMEM((near, group // 2, rows, lanes), i16),
+            pltpu.VMEM((near, group // 2, 2, lanes), f32),
+            pltpu.VMEM((near, group // 2, 2, lanes), f32),
+            pltpu.VMEM((waves, group, rows, lanes), i16),
+            pltpu.VMEM((n_dp, share, rows, lanes), i16),
+            pltpu.VMEM((waves, group, 2, lanes), f32),
+            pltpu.VMEM((n_dp, share, 2, lanes), f32),
+            pltpu.SemaphoreType.DMA((DEPTH,)),
+            pltpu.SemaphoreType.DMA((2, tasks)),
+            pltpu.SemaphoreType.DMA((2, near)),
+            pltpu.SemaphoreType.DMA((2, near)),
+            pltpu.SemaphoreType.DMA((2, n_dp)),
+            pltpu.SemaphoreType.DMA((2, n_dp)),
         ],
         compiler_params=pltpu.CompilerParams(collective_id=0, has_side_effects=True, vmem_limit_bytes=60 << 20),
     )(projected, weights)

time: 136 us -> 112 us (0.82)
  Pallas kernels: 133 us -> 108 us
    pallas_call x1, Pallas kernels: 79.6 us -> 54 us  [gram_sums(): pl.pallas_call(functools.partial(scatter_kernel, n_head, n_dp, share, wav...]
where the time goes in v2:
time: 112 us; the launch traced here: 111 us
  Pallas kernels  108 us (96%)
  other arithmetic  2.01 us (2%)
    pallas_call x1, Pallas kernels, gram_sums(): pl.pallas_call(functools.partial(scatter_kernel, n_head, n_dp, share, wav...  54 us
    pallas_call x1, Pallas kernels, whiten(): pl.pallas_call(functools.partial(whiten_kernel, total, count), in_specs=[...  26.1 us
    pallas_call x1, Pallas kernels, gather(): pl.pallas_call(functools.partial(gather_kernel, n_dp, share), in_specs=[p...  22.1 us
    pallas_call x1, Pallas kernels, unpack(): pl.pallas_call(unpack_kernel, grid=(mats // group,), in_specs=[pl.BlockSp...  5.79 us

profile of v2, /device:TPU:24, one launch (start us, length us, event | category | flops | bytes accessed | tf_op | source)
XLA Modules:
  0.0 110.7 jit_solution(18141274645729815072)
XLA Ops:
  0.0 1.3 %multiply_exponential_fusion.damp_ref = f32[4]{0:T(128)} fusion(s32[128]{0:T(128)} %param.5, s32[]{:T(128)S(6)} %select_n.3), kind=kLoop, calls=%fused_computation.1 | loop fusion | flops 12 | bytes 36 | tf_op jit(solution)/shard_map/exp2 | solution.py:504
  1.3 0.7 exponential_convert_fusion
  2.0 0.8 broadcast_in_dim.4.weights_ref
  2.8 54.0 %shard_map.37.packed_ref = f32[4,192,128]{2,1,0:T(8,128)} custom-call(bf16[384,24576]{1,0:T(8,128)(2,1)} %rows_ref.1, bf16[384,1]{1,0:T(8,128)(2,1)} %broadcast_in_dim.4.weights_ref), custom_call_target="tpu_custom_call" | custom-call | tf_op jit(solution)/shard_map/pallas_call | solution.py:398
  56.7 26.1 %shard_map.38 = (s16[4,192,128]{2,1,0:T(8,128)(2,1)}, f32[4,1,128]{2,1,0:T(1,128)}) custom-call(f32[4]{0:T(128)} %multiply_exponential_fusion.damp_ref, f32[4,192,128]{2,1,0:T(8,128)} %shard_map.37.packed_ref), custom_call_target="tpu_custom_call" | custom-call | tf_op jit(solution)/shard_map/pallas_call | solution.py:142
  82.8 22.1 %shard_map.39 = (s16[16,192,128]{2,1,0:T(8,128)(2,1)}, f32[16,1,128]{2,1,0:T(1,128)}) custom-call(s16[4,192,128]{2,1,0:T(8,128)(2,1)} %get-tuple-element.9.code_ref, f32[4,1,128]{2,1,0:T(1,128)} %get-tuple-element.10.step_ref), custom_call_target="tpu_custom_call" | custom-call | tf_op jit(solution)/shard_map/pallas_call | solution.py:451
  104.9 5.8 %shard_map.40 = f32[16,192,192]{2,1,0:T(8,128)} custom-call(s16[16,192,128]{2,1,0:T(8,128)(2,1)} %get-tuple-element.11.code_ref, f32[16,1,128]{2,1,0:T(1,128)} %get-tuple-element.12.step_ref), custom_call_target="tpu_custom_call" | custom-call | tf_op jit(solution)/shard_map/pallas_call | solution.py:483

commit v3 on v2

--- a/solution.py
+++ b/solution.py
@@ -10,11 +10,11 @@
 
 HD = 192
 BLK = HD // 3
-HIGH = lax.Precision.HIGHEST
 LEVELS = 32767.0
 TINY = 1e-30
 DEPTH = 4
-LAG = 3
+LAG = 2
+RANK = 8
 
 
 def store_pair(rows, wide, out, at):
@@ -33,38 +33,57 @@
     out[at + 1, two:, :] = jnp.where(lanes < BLK, corner, second[HD:, two:])
 
 
+def split(a):
+    high = a.astype(jnp.bfloat16)
+    return high, (a - high.astype(jnp.float32)).astype(jnp.bfloat16)
+
+
+def product(a, b, axis):
+    (a_high, a_low), (b_high, b_low) = split(a), split(b)
+    one = functools.partial(
+        lax.dot_general, dimension_numbers=(((1,), (axis,)), ((), ())), preferred_element_type=jnp.float32
+    )
+    return one(a_high, b_high) + (one(a_high, b_low) + one(a_low, b_high))
+
+
 def dot(a, b):
-    return lax.dot_general(a, b, (((1,), (0,)), ((), ())), precision=HIGH, preferred_element_type=jnp.float32)
+    return product(a, b, 0)
 
 
 def dot_t(a, b):
-    return lax.dot_general(a, b, (((1,), (1,)), ((), ())), precision=HIGH, preferred_element_type=jnp.float32)
+    return product(a, b, 1)
 
 
 def inverse_factors(blocks):
     lane = lax.broadcasted_iota(jnp.int32, (8, BLK), 1)
     sub = lax.broadcasted_iota(jnp.int32, (8, BLK), 0)
-    sub1 = lax.broadcasted_iota(jnp.int32, (8, 1), 0)
     groups = BLK // 8
     held = [[block[8 * g : 8 * g + 8] for g in range(groups)] for block in blocks]
-    for k in range(BLK):
-        own, spot = divmod(k, 8)
-        is_k = lane == k
-        for parts in held:
-            row = parts[own][spot : spot + 1, :]
-            scale = 1.0 / row[:, k : k + 1]
-            row = jnp.where(is_k[:1], 1.0, row) * scale
-            for g in range(own, groups):
-                part = parts[g]
-                column = part[:, k : k + 1]
-                if g == own:
-                    if spot == 7:
-                        continue
-                    column = jnp.where(sub1 > spot, column, 0.0)
-                    kept = jnp.where(is_k & (sub > spot), 0.0, part)
-                else:
-                    kept = jnp.where(is_k, 0.0, part)
-                parts[g] = kept - column * row
+    for start in range(0, BLK, RANK):
+        own, base = divmod(start, 8)
+        spread = [
+            [[jnp.broadcast_to(part[:, start + r : start + r + 1], part.shape) for r in range(RANK)] for part in parts[own:]]
+            for parts in held
+        ]
+        for r in range(RANK):
+            spot = base + r
+            is_k = lane == start + r
+            for parts, columns in zip(held, spread):
+                scale = 1.0 / columns[0][r][spot : spot + 1]
+                row = jnp.where(is_k[:1], 1.0, parts[own][spot : spot + 1]) * scale
+                ahead = [columns[0][q][spot : spot + 1] * scale for q in range(r + 1, RANK)]
+                for g in range(own, groups):
+                    part, column = parts[g], columns[g - own][r]
+                    if g == own:
+                        if spot == 7:
+                            continue
+                        column = jnp.where(sub > spot, column, 0.0)
+                        kept = jnp.where(is_k & (sub > spot), 0.0, part)
+                    else:
+                        kept = jnp.where(is_k, 0.0, part)
+                    parts[g] = kept - column * row
+                    for q, factor in enumerate(ahead, r + 1):
+                        columns[g - own][q] -= column * factor
     out = []
     for parts in held:
         rows = []
@@ -95,61 +114,6 @@
     return code.astype(jnp.int32).astype(jnp.float32)
 
 
-def whiten_kernel(total, count, damp_ref, packed_ref, out_ref, step_ref):
-    two = 2 * BLK
-    diag = lax.broadcasted_iota(jnp.int32, (BLK, BLK), 0) == lax.broadcasted_iota(jnp.int32, (BLK, BLK), 1)
-    a11, a22, a33, low, a32 = [], [], [], [], []
-    for m in range(count):
-        got = packed_ref[m] / total
-        even = unpack_even(got)
-        odd = unpack_odd(got)
-        if count % 2 == 0:
-            d1, d2, d3, left, corner = odd if m % 2 else even
-        else:
-            turn = (lax.axis_index("head") * lax.axis_size("dp") + lax.axis_index("dp")) * count + m
-            d1, d2, d3, left, corner = (jnp.where(turn % 2 == 0, a, b) for a, b in zip(even, odd))
-        trace = jnp.sum(jnp.where(diag, d1 + d2 + d3, 0.0), axis=(0, 1), keepdims=True)
-        level = trace / HD + 1e-06
-        shift = jnp.where(diag, damp_ref[m] * level, 0.0)
-        a11.append(d1 + shift)
-        a22.append(d2 + shift)
-        a33.append(d3 + shift)
-        low.append(left)
-        a32.append(corner)
-    each = range(count)
-    w11 = inverse_factors(a11)
-    l1 = [dot_t(low[m], w11[m]) for m in each]
-    square = [dot_t(l1[m], l1[m]) for m in each]
-    w22 = inverse_factors([a22[m] - square[m][:BLK, :BLK] for m in each])
-    l32 = [dot_t(a32[m] - square[m][BLK:, :BLK], w22[m]) for m in each]
-    w33 = inverse_factors([a33[m] - square[m][BLK:, BLK:] - dot_t(l32[m], l32[m]) for m in each])
-    for m in each:
-        below = dot(l1[m], w11[m])
-        w21 = -dot(w22[m], below[:BLK])
-        w32 = -dot(w33[m], dot(l32[m], w22[m]))
-        w31 = -dot(w33[m], below[BLK:] + dot(l32[m], w21))
-        bands = ((w11[m], w33[m]), (w21, w22[m]), (w31, w32))
-        bands = [jnp.concatenate(band, axis=1) for band in bands]
-        top = functools.reduce(jnp.maximum, [jnp.max(jnp.abs(band), axis=0, keepdims=True) for band in bands])
-        top = jnp.maximum(top, TINY)
-        step_ref[m] = top / LEVELS
-        for n, band in enumerate(bands):
-            out_ref[m, n * BLK : (n + 1) * BLK] = encode(band, LEVELS / top)
-
-
-def whiten(packed, damp, total):
-    count = packed.shape[0]
-    return pl.pallas_call(
-        functools.partial(whiten_kernel, total, count),
-        in_specs=[pl.BlockSpec(memory_space=pltpu.SMEM), pl.BlockSpec(memory_space=pltpu.VMEM)],
-        out_specs=[pl.BlockSpec(memory_space=pltpu.VMEM)] * 2,
-        out_shape=[
-            jax.ShapeDtypeStruct(packed.shape, jnp.int16),
-            jax.ShapeDtypeStruct((count, 1, packed.shape[2]), jnp.float32),
-        ],
-    )(damp, packed)
-
-
 def flip(index, step):
     return index + step * (1 - 2 * ((index // step) % 2))
 
@@ -165,13 +129,113 @@
     )
 
 
+def signal(device):
+    barrier = pltpu.get_barrier_semaphore()
+    pl.semaphore_signal(barrier, inc=1, device_id=device, device_id_type=pl.DeviceIdType.MESH)
+
+
 def greet(heads, dps):
-    barrier = pltpu.get_barrier_semaphore()
     for peer in heads:
-        pl.semaphore_signal(barrier, inc=1, device_id={"head": peer}, device_id_type=pl.DeviceIdType.MESH)
+        signal({"head": peer})
     for peer in dps:
-        pl.semaphore_signal(barrier, inc=1, device_id={"dp": peer}, device_id_type=pl.DeviceIdType.MESH)
-    pl.semaphore_wait(barrier, len(heads) + len(dps))
+        signal({"dp": peer})
+    pl.semaphore_wait(pltpu.get_barrier_semaphore(), len(heads) + len(dps))
+
+
+def whiten_kernel(total, n_dp, count, damp_ref, packed_ref, codes, steps, sems, step_sems):
+    two = 2 * BLK
+    dp = lax.axis_index("dp")
+    peers = [lax.rem(dp + o, n_dp) for o in range(1, n_dp)]
+    for peer in peers:
+        signal({"dp": peer})
+    pairs = (count + 1) // 2
+    edges = (0, pairs, pairs + count, 2 * (pairs + count))
+    diag = lax.broadcasted_iota(jnp.int32, (BLK, BLK), 0) == lax.broadcasted_iota(jnp.int32, (BLK, BLK), 1)
+    first = (lax.axis_index("head") * n_dp + dp) * count
+    a11, a22, a33, low, a32 = [], [], [], [], []
+    for m in range(count):
+        got = packed_ref[m] / total
+        even = unpack_even(got)
+        odd = unpack_odd(got)
+        if count % 2 == 0:
+            d1, d2, d3, left, corner = odd if m % 2 else even
+        else:
+            d1, d2, d3, left, corner = (jnp.where((first + m) % 2 == 0, a, b) for a, b in zip(even, odd))
+        trace = jnp.sum(jnp.where(diag, d1 + d2 + d3, 0.0), axis=(0, 1), keepdims=True)
+        level = trace / HD + 1e-06
+        damping = jnp.exp2(-jnp.full((1, 1), damp_ref[first + m]).astype(jnp.float32))
+        shift = jnp.where(diag, damping * level, 0.0)
+        a11.append(d1 + shift)
+        a22.append(d2 + shift)
+        a33.append(d3 + shift)
+        low.append(left)
+        a32.append(corner)
+    each = range(count)
+
+    def put(n, left, right):
+        block = jnp.concatenate((left, right), axis=1)
+        top = jnp.maximum(jnp.max(jnp.abs(block), axis=0, keepdims=True), TINY)
+        steps[dp, n] = top / LEVELS
+        codes[dp, n * BLK : (n + 1) * BLK] = encode(block, LEVELS / top)
+
+    def put_pairs(n, values):
+        for p in range(pairs):
+            put(n + p, values[2 * p], values[min(2 * p + 1, count - 1)])
+
+    flight = []
+
+    def send(stage):
+        blocks = pl.ds(edges[stage], edges[stage + 1] - edges[stage])
+        rows = pl.ds(edges[stage] * BLK, (edges[stage + 1] - edges[stage]) * BLK)
+        for o, peer in enumerate(peers):
+            slot = stage * len(peers) + o
+            code, step = codes.at[dp, rows], steps.at[dp, blocks]
+            flight.append(remote(code, code, sems, slot, {"dp": peer}))
+            flight.append(remote(step, step, step_sems, slot, {"dp": peer}))
+        for copy in flight[-2 * len(peers) :]:
+            copy.start()
+
+    w11 = inverse_factors(a11)
+    put_pairs(0, w11)
+    pl.semaphore_wait(pltpu.get_barrier_semaphore(), len(peers))
+    send(0)
+    l1 = [dot_t(low[m], w11[m]) for m in each]
+    square = [dot_t(l1[m], l1[m]) for m in each]
+    w22 = inverse_factors([a22[m] - square[m][:BLK, :BLK] for m in each])
+    below = [dot(l1[m], w11[m]) for m in each]
+    w21 = [-dot(w22[m], below[m][:BLK]) for m in each]
+    for m in each:
+        put(edges[1] + m, w21[m], w22[m])
+    send(1)
+    l32 = [dot_t(a32[m] - square[m][BLK:, :BLK], w22[m]) for m in each]
+    w33 = inverse_factors([a33[m] - square[m][BLK:, BLK:] - dot_t(l32[m], l32[m]) for m in each])
+    put_pairs(edges[2] + count, w33)
+    for m in each:
+        w32 = -dot(w33[m], dot(l32[m], w22[m]))
+        w31 = -dot(w33[m], below[m][BLK:] + dot(l32[m], w21[m]))
+        put(edges[2] + m, w31, w32)
+    send(2)
+    for copy in flight:
+        copy.wait()
+
+
+def whiten(packed, damp, n_dp, total):
+    count, _, lanes = packed.shape
+    blocks = 2 * ((count + 1) // 2 + count)
+    return pl.pallas_call(
+        functools.partial(whiten_kernel, total, n_dp, count),
+        in_specs=[pl.BlockSpec(memory_space=pltpu.SMEM), pl.BlockSpec(memory_space=pltpu.VMEM)],
+        out_specs=[pl.BlockSpec(memory_space=pltpu.VMEM)] * 2,
+        out_shape=[
+            jax.ShapeDtypeStruct((n_dp, blocks * BLK, lanes), jnp.int16),
+            jax.ShapeDtypeStruct((n_dp, blocks, 1, lanes), jnp.float32),
+        ],
+        scratch_shapes=[
+            pltpu.SemaphoreType.DMA((2, 3 * (n_dp - 1))),
+            pltpu.SemaphoreType.DMA((2, 3 * (n_dp - 1))),
+        ],
+        compiler_params=pltpu.CompilerParams(collective_id=1, has_side_effects=True),
+    )(damp, packed)
 
 
 def outer_steps(t, u, odd):
@@ -263,7 +327,12 @@
 
     for v in range(DEPTH - 1):
         fetch(v).start()
-    wide[...] = jnp.broadcast_to(weights_ref[...], wide.shape)
+    two = 2 * BLK
+    for n in range(weights_ref.shape[0]):
+        row = jnp.exp2(weights_ref[n : n + 1].astype(jnp.float32))
+        column = jnp.broadcast_to(row, (two, two)).T.astype(wide.dtype)
+        for lanes in range(0, 2 * HD, two):
+            wide[n * two : (n + 1) * two, lanes : lanes + two] = column
     greet([flip(head, 1 << j) for j in range(bits + 1)], peers)
 
     def multiply(v, out):
@@ -339,7 +408,7 @@
     for k, (w, e) in enumerate(tasks):
         for odd in (0, 1):
             waits = len(receipts(e, odd))
-            at = k + 1 if not waits else k + LAG * waits
+            at = k + 2 + LAG * waits
             plan.setdefault(at, []).append((k, odd))
     swapped = set()
     far = []
@@ -425,86 +494,49 @@
     )(projected, weights)
 
 
-def gather_kernel(n_dp, share, code_ref, step_ref, codes, steps, sems, step_sems, own_sems):
-    dp = lax.axis_index("dp")
-    peers = [lax.rem(dp + o, n_dp) for o in range(1, n_dp)]
-    mine = pl.ds(dp * share, share)
-    own = [
-        pltpu.make_async_copy(code_ref, codes.at[mine], own_sems.at[0]),
-        pltpu.make_async_copy(step_ref, steps.at[mine], own_sems.at[1]),
-    ]
-    for copy in own:
-        copy.start()
-    greet([], peers)
-    flight = []
-    for o, peer in enumerate(peers):
-        flight.append(remote(code_ref, codes.at[mine], sems, o, {"dp": peer}))
-        flight.append(remote(step_ref, steps.at[mine], step_sems, o, {"dp": peer}))
-    for copy in flight:
-        copy.start()
-    for copy in own + flight:
-        copy.wait()
-
-
-def gather(code, step, n_dp):
-    share = code.shape[0]
+def unpack_kernel(count, code_ref, step_ref, out_ref):
+    two = 2 * BLK
+    pairs = (count + 1) // 2
+    left = lax.broadcasted_iota(jnp.int32, (BLK, two), 1) < BLK
+    for d in range(code_ref.shape[0]):
+
+        def block(n, d=d):
+            return decode(code_ref[d, n * BLK : (n + 1) * BLK]) * step_ref[d, n]
+
+        for m in range(count):
+            at = d * count + m
+            top, last = block(m // 2), block(2 * pairs + 2 * count - pairs + m // 2)
+            if m % 2:
+                top, last = pltpu.roll(top, BLK, 1), pltpu.roll(last, BLK, 1)
+            out_ref[at, :BLK, :two] = jnp.where(left, top, 0.0)
+            out_ref[at, BLK:two, :two] = block(pairs + m)
+            out_ref[at, two:, :two] = block(pairs + count + m)
+            out_ref[at, :two, two:] = jnp.zeros((two, BLK), jnp.float32)
+            out_ref[at, two:, two:] = last[:, :BLK]
+
+
+def unpack(codes, steps, count):
+    n_dp, rows, lanes = codes.shape
+    group = n_dp // 2 if n_dp % 2 == 0 else n_dp
     return pl.pallas_call(
-        functools.partial(gather_kernel, n_dp, share),
-        in_specs=[pl.BlockSpec(memory_space=pltpu.VMEM)] * 2,
-        out_specs=[pl.BlockSpec(memory_space=pltpu.VMEM)] * 2,
-        out_shape=[
-            jax.ShapeDtypeStruct((n_dp * share, *code.shape[1:]), code.dtype),
-            jax.ShapeDtypeStruct((n_dp * share, *step.shape[1:]), step.dtype),
-        ],
-        scratch_shapes=[
-            pltpu.SemaphoreType.DMA((2, n_dp - 1)),
-            pltpu.SemaphoreType.DMA((2, n_dp - 1)),
-            pltpu.SemaphoreType.DMA((2,)),
-        ],
-        compiler_params=pltpu.CompilerParams(collective_id=1, has_side_effects=True),
-    )(code, step)
-
-
-def unpack_kernel(code_ref, step_ref, out_ref):
-    two = 2 * BLK
-    left = lax.broadcasted_iota(jnp.int32, (BLK, two), 1) < BLK
-    for m in range(out_ref.shape[0]):
-        step = step_ref[m]
-        top = decode(code_ref[m, :BLK]) * step
-        out_ref[m, :BLK, :two] = jnp.where(left, top, 0.0)
-        out_ref[m, BLK:, :two] = decode(code_ref[m, BLK:]) * step
-        out_ref[m, :two, two:] = jnp.zeros((two, BLK), jnp.float32)
-        out_ref[m, two:, two:] = top[:, BLK:]
-
-
-def unpack(codes, steps):
-    mats, rows, lanes = codes.shape
-    group = 2
-    return pl.pallas_call(
-        unpack_kernel,
-        grid=(mats // group,),
+        functools.partial(unpack_kernel, count),
+        grid=(n_dp // group,),
         in_specs=[
             pl.BlockSpec((group, rows, lanes), lambda i: (i, 0, 0)),
-            pl.BlockSpec((group, 1, lanes), lambda i: (i, 0, 0)),
+            pl.BlockSpec((group, rows // BLK, 1, lanes), lambda i: (i, 0, 0, 0)),
         ],
-        out_specs=pl.BlockSpec((group, HD, HD), lambda i: (i, 0, 0)),
-        out_shape=jax.ShapeDtypeStruct((mats, HD, HD), jnp.float32),
+        out_specs=pl.BlockSpec((group * count, HD, HD), lambda i: (i, 0, 0)),
+        out_shape=jax.ShapeDtypeStruct((n_dp * count, HD, HD), jnp.float32),
     )(codes, steps)
 
 
 def on_device(projected, weight_exp, damp_exp):
     n_head = lax.axis_size("head")
     n_dp = lax.axis_size("dp")
-    mats = projected.shape[1] // HD
-    share = mats // (n_head * n_dp)
     total = projected.shape[0] * n_head * n_dp
-    weights = jnp.exp2(weight_exp.astype(jnp.float32)).astype(jnp.bfloat16)
-    owned = gram_sums(projected, weights[:, None], n_head, n_dp)
-    first = (lax.axis_index("head") * n_dp + lax.axis_index("dp")) * share
-    damp = jnp.exp2(-lax.dynamic_slice_in_dim(damp_exp, first, share, 0).astype(jnp.float32))
-    code, step = whiten(owned, damp, float(total))
-    codes, steps = gather(code, step, n_dp)
-    return unpack(codes, steps)
+    owned = gram_sums(projected, weight_exp.reshape(-1, 2 * BLK), n_head, n_dp)
+    codes, steps = whiten(owned, damp_exp, n_dp, float(total))
+    return unpack(codes, steps, owned.shape[0])
 
 
 def solution(mesh):

time: 112 us -> 77.1 us (0.69)
  Pallas kernels: 108 us -> 75.6 us
  other arithmetic: 2.01 us -> 0 us
    pallas_call x3 -> x2, Pallas kernels: 53.9 us -> 30.7 us  [the longest x1 27.8 us: whiten(): pl.pallas_call(functools.partial(whiten_kernel, total, n_dp, count), in_s...]
    pallas_call x1, Pallas kernels: 54 us -> 45 us  [gram_sums(): pl.pallas_call(functools.partial(scatter_kernel, n_head, n_dp, share, wav...]
    exp2 x1 -> x0, other arithmetic: 1.33 us -> none  [on_device(): jnp.exp2(-lax.dynamic_slice_in_dim(damp_exp, first, share, 0).astype(jnp....]
where the time goes in v3:
time: 77.1 us; the launch traced here: 75.7 us
  Pallas kernels  75.6 us (98%)
    pallas_call x1, Pallas kernels, gram_sums(): pl.pallas_call(functools.partial(scatter_kernel, n_head, n_dp, share, wav...  45 us
    pallas_call x1, Pallas kernels, whiten(): pl.pallas_call(functools.partial(whiten_kernel, total, n_dp, count), in_s...  27.8 us
    pallas_call x1, Pallas kernels, unpack(): pl.pallas_call(functools.partial(unpack_kernel, count), grid=(n_dp // gro...  2.83 us

profile of v3, /device:TPU:24, one launch (start us, length us, event | category | flops | bytes accessed | tf_op | source)
XLA Modules:
  0.0 75.7 jit_solution(16325200066023811462)
XLA Ops:
  0.0 45.0 %shard_map.37.packed_ref = f32[4,192,128]{2,1,0:T(8,128)} custom-call(bf16[384,24576]{1,0:T(8,128)(2,1)} %rows_ref.1, s32[3,128]{1,0:T(4,128)} %bitcast.1), custom_call_target="tpu_custom_call" | custom-call | tf_op jit(solution)/shard_map/pallas_call | solution.py:467
  45.0 27.8 %shard_map.38 = (s16[4,768,128]{2,1,0:T(8,128)(2,1)}, f32[4,12,1,128]{3,2,1,0:T(1,128)}) custom-call(s32[128]{0:T(128)} %damp_ref.1, f32[4,192,128]{2,1,0:T(8,128)} %shard_map.37.packed_ref), custom_call_target="tpu_custom_call" | custom-call | tf_op jit(solution)/shard_map/pallas_call | solution.py:225
  72.8 2.8 %shard_map.39 = f32[16,192,192]{2,1,0:T(8,128)} custom-call(s16[4,768,128]{2,1,0:T(8,128)(2,1)} %get-tuple-element.7.code_ref, f32[4,12,1,128]{3,2,1,0:T(1,128)} %get-tuple-element.8.step_ref), custom_call_target="tpu_custom_call" | custom-call | tf_op jit(solution)/shard_map/pallas_call | solution.py:521

commit v4 on v3

--- a/solution.py
+++ b/solution.py
@@ -15,6 +15,7 @@
 DEPTH = 4
 LAG = 2
 RANK = 8
+HALF = BLK // 2
 
 
 def store_pair(rows, wide, out, at):
@@ -54,12 +55,14 @@
     return product(a, b, 1)
 
 
-def inverse_factors(blocks):
+def inverse_halves(blocks):
     lane = lax.broadcasted_iota(jnp.int32, (8, BLK), 1)
     sub = lax.broadcasted_iota(jnp.int32, (8, BLK), 0)
     groups = BLK // 8
     held = [[block[8 * g : 8 * g + 8] for g in range(groups)] for block in blocks]
     for start in range(0, BLK, RANK):
+        if start == HALF:
+            yield finished(held, 0, groups // 2)
         own, base = divmod(start, 8)
         spread = [
             [[jnp.broadcast_to(part[:, start + r : start + r + 1], part.shape) for r in range(RANK)] for part in parts[own:]]
@@ -84,16 +87,34 @@
                     parts[g] = kept - column * row
                     for q, factor in enumerate(ahead, r + 1):
                         columns[g - own][q] -= column * factor
+    yield finished(held, groups // 2, groups)
+
+
+def finished(held, begin, end):
+    lane = lax.broadcasted_iota(jnp.int32, (8, BLK), 1)
+    sub = lax.broadcasted_iota(jnp.int32, (8, BLK), 0)
     out = []
     for parts in held:
         rows = []
-        for g in range(groups):
+        for g in range(begin, end):
             ids = sub + 8 * g
             pivot = jnp.sum(jnp.where(lane == ids, parts[g], 0.0), axis=1, keepdims=True)
             unit = jnp.where(lane < ids, parts[g], jnp.where(lane == ids, 1.0, 0.0))
             rows.append(unit * (1.0 / jnp.sqrt(pivot)))
         out.append(jnp.concatenate(rows, axis=0))
     return out
+
+
+def stage_starts(count):
+    pairs = (count + 1) // 2
+    starts = [0]
+    for cells in (pairs, pairs, count, count, count + pairs, count + pairs):
+        starts.append(starts[-1] + cells)
+    return starts
+
+
+def joined(halves):
+    return [jnp.concatenate(both, axis=0) for both in zip(*halves)]
 
 
 def unpack_even(got):
@@ -142,14 +163,11 @@
     pl.semaphore_wait(pltpu.get_barrier_semaphore(), len(heads) + len(dps))
 
 
-def whiten_kernel(total, n_dp, count, damp_ref, packed_ref, codes, steps, sems, step_sems):
-    two = 2 * BLK
+def whiten_owned(total, n_dp, count, damp_ref, packed_ref, codes, steps, sems, step_sems):
     dp = lax.axis_index("dp")
     peers = [lax.rem(dp + o, n_dp) for o in range(1, n_dp)]
-    for peer in peers:
-        signal({"dp": peer})
     pairs = (count + 1) // 2
-    edges = (0, pairs, pairs + count, 2 * (pairs + count))
+    starts = stage_starts(count)
     diag = lax.broadcasted_iota(jnp.int32, (BLK, BLK), 0) == lax.broadcasted_iota(jnp.int32, (BLK, BLK), 1)
     first = (lax.axis_index("head") * n_dp + dp) * count
     a11, a22, a33, low, a32 = [], [], [], [], []
@@ -176,7 +194,7 @@
         block = jnp.concatenate((left, right), axis=1)
         top = jnp.maximum(jnp.max(jnp.abs(block), axis=0, keepdims=True), TINY)
         steps[dp, n] = top / LEVELS
-        codes[dp, n * BLK : (n + 1) * BLK] = encode(block, LEVELS / top)
+        codes[dp, n * HALF : (n + 1) * HALF] = encode(block, LEVELS / top)
 
     def put_pairs(n, values):
         for p in range(pairs):
@@ -185,8 +203,9 @@
     flight = []
 
     def send(stage):
-        blocks = pl.ds(edges[stage], edges[stage + 1] - edges[stage])
-        rows = pl.ds(edges[stage] * BLK, (edges[stage + 1] - edges[stage]) * BLK)
+        cells = starts[stage + 1] - starts[stage]
+        blocks = pl.ds(starts[stage], cells)
+        rows = pl.ds(starts[stage] * HALF, cells * HALF)
         for o, peer in enumerate(peers):
             slot = stage * len(peers) + o
             code, step = codes.at[dp, rows], steps.at[dp, blocks]
@@ -195,47 +214,35 @@
         for copy in flight[-2 * len(peers) :]:
             copy.start()
 
-    w11 = inverse_factors(a11)
-    put_pairs(0, w11)
-    pl.semaphore_wait(pltpu.get_barrier_semaphore(), len(peers))
-    send(0)
+    halves = []
+    for h, half in enumerate(inverse_halves(a11)):
+        put_pairs(starts[h], half)
+        send(h)
+        halves.append(half)
+    w11 = joined(halves)
     l1 = [dot_t(low[m], w11[m]) for m in each]
     square = [dot_t(l1[m], l1[m]) for m in each]
-    w22 = inverse_factors([a22[m] - square[m][:BLK, :BLK] for m in each])
     below = [dot(l1[m], w11[m]) for m in each]
-    w21 = [-dot(w22[m], below[m][:BLK]) for m in each]
-    for m in each:
-        put(edges[1] + m, w21[m], w22[m])
-    send(1)
+    halves, lefts = [], []
+    for h, half in enumerate(inverse_halves([a22[m] - square[m][:BLK, :BLK] for m in each])):
+        left = [-dot(half[m], below[m][:BLK]) for m in each]
+        for m in each:
+            put(starts[2 + h] + m, left[m], half[m])
+        send(2 + h)
+        halves.append(half)
+        lefts.append(left)
+    w22, w21 = joined(halves), joined(lefts)
     l32 = [dot_t(a32[m] - square[m][BLK:, :BLK], w22[m]) for m in each]
-    w33 = inverse_factors([a33[m] - square[m][BLK:, BLK:] - dot_t(l32[m], l32[m]) for m in each])
-    put_pairs(edges[2] + count, w33)
-    for m in each:
-        w32 = -dot(w33[m], dot(l32[m], w22[m]))
-        w31 = -dot(w33[m], below[m][BLK:] + dot(l32[m], w21[m]))
-        put(edges[2] + m, w31, w32)
-    send(2)
+    right = [dot(l32[m], w22[m]) for m in each]
+    left = [below[m][BLK:] + dot(l32[m], w21[m]) for m in each]
+    rest = [a33[m] - square[m][BLK:, BLK:] - dot_t(l32[m], l32[m]) for m in each]
+    for h, half in enumerate(inverse_halves(rest)):
+        for m in each:
+            put(starts[4 + h] + m, -dot(half[m], left[m]), -dot(half[m], right[m]))
+        put_pairs(starts[4 + h] + count, half)
+        send(4 + h)
     for copy in flight:
         copy.wait()
-
-
-def whiten(packed, damp, n_dp, total):
-    count, _, lanes = packed.shape
-    blocks = 2 * ((count + 1) // 2 + count)
-    return pl.pallas_call(
-        functools.partial(whiten_kernel, total, n_dp, count),
-        in_specs=[pl.BlockSpec(memory_space=pltpu.SMEM), pl.BlockSpec(memory_space=pltpu.VMEM)],
-        out_specs=[pl.BlockSpec(memory_space=pltpu.VMEM)] * 2,
-        out_shape=[
-            jax.ShapeDtypeStruct((n_dp, blocks * BLK, lanes), jnp.int16),
-            jax.ShapeDtypeStruct((n_dp, blocks, 1, lanes), jnp.float32),
-        ],
-        scratch_shapes=[
-            pltpu.SemaphoreType.DMA((2, 3 * (n_dp - 1))),
-            pltpu.SemaphoreType.DMA((2, 3 * (n_dp - 1))),
-        ],
-        compiler_params=pltpu.CompilerParams(collective_id=1, has_side_effects=True),
-    )(damp, packed)
 
 
 def outer_steps(t, u, odd):
@@ -291,7 +298,7 @@
     return next((s for s, j in enumerate(order) if (e >> j) & 1), len(order))
 
 
-def scatter_kernel(n_head, n_dp, share, waves, rows_ref, weights_ref, out_ref, acc, half, sent, wide, columns, code_out, code_in, step_out, step_in, far_out, far_in, far_step_out, far_step_in, sem_in, sem_0, sem_code, sem_step, sem_far, sem_far_step):
+def scatter_kernel(n_head, n_dp, share, waves, total_tokens, rows_ref, weights_ref, damp_ref, codes, steps, owned, acc, half, sent, wide, columns, code_out, code_in, step_out, step_in, far_out, far_in, far_step_out, far_step_in, sem_in, sem_0, sem_code, sem_step, sem_far, sem_far_step, sem_out, sem_out_step):
     head = lax.axis_index("head")
     dp = lax.axis_index("dp")
     chunks = n_head // 2
@@ -433,7 +440,7 @@
         value = acc[last, place * share + m]
         for slot in slots:
             value += get_code_either(odd, far_in, far_step_in, slot, m)
-        out_ref[m] = value
+        owned[m] = value
         return carry
 
     if share % 2:
@@ -444,6 +451,7 @@
             return total(2 * i + 1, total(2 * i, carry, 0), 1)
 
         lax.fori_loop(0, share // 2, both, 0, unroll=True)
+    whiten_owned(total_tokens, n_dp, share, damp_ref, owned, codes, steps, sem_out, sem_out_step)
 
 
 def wave_count(per_head, n_dp):
@@ -453,7 +461,7 @@
     return waves
 
 
-def gram_sums(projected, weights, n_head, n_dp):
+def whitened_codes(projected, weights, damp, n_head, n_dp):
     tokens, width = projected.shape
     mats, rows, lanes = width // HD, HD, 2 * BLK
     per_head = mats // n_head
@@ -463,13 +471,18 @@
     group = per_head // waves
     tasks = waves * chunks
     near = 2 * waves * (chunks - 1)
+    cells = stage_starts(share)[-1]
     f32, i16 = jnp.float32, jnp.int16
     return pl.pallas_call(
-        functools.partial(scatter_kernel, n_head, n_dp, share, waves),
-        in_specs=[pl.BlockSpec(memory_space=pl.ANY), pl.BlockSpec(memory_space=pltpu.VMEM)],
-        out_specs=pl.BlockSpec(memory_space=pltpu.VMEM),
-        out_shape=jax.ShapeDtypeStruct((share, rows, lanes), f32),
+        functools.partial(scatter_kernel, n_head, n_dp, share, waves, float(tokens * n_head * n_dp)),
+        in_specs=[pl.BlockSpec(memory_space=space) for space in (pl.ANY, pltpu.VMEM, pltpu.SMEM)],
+        out_specs=[pl.BlockSpec(memory_space=pltpu.VMEM)] * 2,
+        out_shape=[
+            jax.ShapeDtypeStruct((n_dp, cells * HALF, lanes), i16),
+            jax.ShapeDtypeStruct((n_dp, cells, 1, lanes), f32),
+        ],
         scratch_shapes=[
+            pltpu.VMEM((share, rows, lanes), f32),
             pltpu.VMEM((tasks, group, rows, lanes), f32),
             pltpu.VMEM((tasks, group, rows, lanes), f32),
             pltpu.VMEM((tasks, group, rows, lanes), f32),
@@ -489,28 +502,32 @@
             pltpu.SemaphoreType.DMA((2, near)),
             pltpu.SemaphoreType.DMA((2, n_dp)),
             pltpu.SemaphoreType.DMA((2, n_dp)),
+            pltpu.SemaphoreType.DMA((2, 6 * (n_dp - 1))),
+            pltpu.SemaphoreType.DMA((2, 6 * (n_dp - 1))),
         ],
         compiler_params=pltpu.CompilerParams(collective_id=0, has_side_effects=True, vmem_limit_bytes=60 << 20),
-    )(projected, weights)
+    )(projected, weights, damp)
 
 
 def unpack_kernel(count, code_ref, step_ref, out_ref):
     two = 2 * BLK
-    pairs = (count + 1) // 2
+    starts = stage_starts(count)
     left = lax.broadcasted_iota(jnp.int32, (BLK, two), 1) < BLK
     for d in range(code_ref.shape[0]):
 
-        def block(n, d=d):
-            return decode(code_ref[d, n * BLK : (n + 1) * BLK]) * step_ref[d, n]
+        def block(stage, n, d=d):
+            cells = [starts[stage + h] + n for h in range(2)]
+            parts = [decode(code_ref[d, c * HALF : (c + 1) * HALF]) * step_ref[d, c] for c in cells]
+            return jnp.concatenate(parts, axis=0)
 
         for m in range(count):
             at = d * count + m
-            top, last = block(m // 2), block(2 * pairs + 2 * count - pairs + m // 2)
+            top, last = block(0, m // 2), block(4, count + m // 2)
             if m % 2:
                 top, last = pltpu.roll(top, BLK, 1), pltpu.roll(last, BLK, 1)
             out_ref[at, :BLK, :two] = jnp.where(left, top, 0.0)
-            out_ref[at, BLK:two, :two] = block(pairs + m)
-            out_ref[at, two:, :two] = block(pairs + count + m)
+            out_ref[at, BLK:two, :two] = block(2, m)
+            out_ref[at, two:, :two] = block(4, m)
             out_ref[at, :two, two:] = jnp.zeros((two, BLK), jnp.float32)
             out_ref[at, two:, two:] = last[:, :BLK]
 
@@ -523,7 +540,7 @@
         grid=(n_dp // group,),
         in_specs=[
             pl.BlockSpec((group, rows, lanes), lambda i: (i, 0, 0)),
-            pl.BlockSpec((group, rows // BLK, 1, lanes), lambda i: (i, 0, 0, 0)),
+            pl.BlockSpec((group, rows // HALF, 1, lanes), lambda i: (i, 0, 0, 0)),
         ],
         out_specs=pl.BlockSpec((group * count, HD, HD), lambda i: (i, 0, 0)),
         out_shape=jax.ShapeDtypeStruct((n_dp * count, HD, HD), jnp.float32),
@@ -533,10 +550,9 @@
 def on_device(projected, weight_exp, damp_exp):
     n_head = lax.axis_size("head")
     n_dp = lax.axis_size("dp")
-    total = projected.shape[0] * n_head * n_dp
-    owned = gram_sums(projected, weight_exp.reshape(-1, 2 * BLK), n_head, n_dp)
-    codes, steps = whiten(owned, damp_exp, n_dp, float(total))
-    return unpack(codes, steps, owned.shape[0])
+    share = projected.shape[1] // HD // (n_head * n_dp)
+    codes, steps = whitened_codes(projected, weight_exp.reshape(-1, 2 * BLK), damp_exp, n_head, n_dp)
+    return unpack(codes, steps, share)
 
 
 def solution(mesh):

time: 77.1 us -> 73.8 us (0.957)
  the two profiles are of different devices: /device:TPU:24 before, /device:TPU:0 now
where the time goes in v4:
time: 73.8 us; the launch traced here: 73.6 us
  Pallas kernels  73.6 us (100%)
    pallas_call x1, Pallas kernels, whitened_codes(): pl.pallas_call(functools.partial(scatter_kernel, n_head, n_dp, share, wav...  70.8 us
    pallas_call x1, Pallas kernels, unpack(): pl.pallas_call(functools.partial(unpack_kernel, count), grid=(n_dp // gro...  2.83 us

profile of v4, /device:TPU:0, one launch (start us, length us, event | category | flops | bytes accessed | tf_op | source)
XLA Modules:
  0.0 73.6 jit_solution(16987480371501966784)
XLA Ops:
  0.0 70.8 %shard_map.37 = (s16[4,768,128]{2,1,0:T(8,128)(2,1)}, f32[4,24,1,128]{3,2,1,0:T(1,128)}) custom-call(bf16[384,24576]{1,0:T(8,128)(2,1)} %rows_ref.1, s32[3,128]{1,0:T(4,128)} %bitcast.1, s32[128]{0:T(128)} %damp_ref.1), custom_call_target="tpu_custom_call" | custom-call | tf_op jit(solution)/shard_map/pallas_call | solution.py:476
  70.8 2.8 %shard_map.38 = f32[16,192,192]{2,1,0:T(8,128)} custom-call(s16[4,768,128]{2,1,0:T(8,128)(2,1)} %get-tuple-element.7.code_ref, f32[4,24,1,128]{3,2,1,0:T(1,128)} %get-tuple-element.8.step_ref), custom_call_target="tpu_custom_call" | custom-call | tf_op jit(solution)/shard_map/pallas_call | solution.py:538
